TPU v7x, 256 devices: a whole 4x4x8 slice. The times are simulated.
256 devices in a mesh: rep: 16 (over y, z_hi, core), tp: 16 (over x, z_lo).
Axes of the slice: x: 4, y: 4, z: 8 (z_hi: 2, z_lo: 4; z = z_hi * 4 + z_lo), core: 2. Of those that a mesh axis runs over, the one named last changes fastest.
Arguments:
- activations: bfloat16 [16, 2048, 4096], P('rep', 'tp'), may hold values from -6 to 6
- cotangent: bfloat16 [16, 2048, 8192], P('rep', None, 'tp'), may hold values from -0.13183594 to 0.13183594
- drift: bfloat16 [16, 4096, 8192], P('rep', None, 'tp'), may hold values from -8 to 8
- outer_weights: float32 [4096, 8192], P(('rep', 'tp')), may hold values from -6 to 6
- momentum: float32 [4096, 8192], P(('rep', 'tp')), may hold values from -6 to 6
Outputs:
- weights: bfloat16 [4096, 8192], P(None, 'tp')
- new_outer: float32 [4096, 8192], P(('rep', 'tp'))
- new_momentum: float32 [4096, 8192], P(('rep', 'tp'))
All inputs are finite; a program needn't handle non-finite values.
Results may differ from a plain program's by a relative error of at most 0.0085.
Values may be sent and summed in bfloat16 or wider, within the bound.
A program may use at most 128 MiB of HBM per device.

v0:
```python
import jax
import jax.numpy as jnp
from jax import lax
from jax.sharding import Mesh
from jax.sharding import PartitionSpec as P

TP = ("tp_0", "tp_1")
REP_TP = ("rep", "tp_0", "tp_1")
outer_rate = 0.7
nesterov = 0.9


def gathered_by_axis(shard, axes, dim):
    if not axes:
        return shard
    nearer = lax.all_gather(shard, axes[-1], axis=dim, tiled=True)
    return gathered_by_axis(nearer, axes[:-1], dim)


def on_device(activations, cotangent, drift, outer_weights, momentum):
    replicas = lax.axis_size("rep")
    cot_rows = cotangent[0]
    grad = jnp.einsum(
        "td,tf->df",
        gathered_by_axis(activations, TP, 1)[0],
        cot_rows,
        preferred_element_type=jnp.float32,
    )
    delta = lax.optimization_barrier((drift[0].astype(jnp.float32) + grad).astype(jnp.bfloat16))
    summed = lax.psum_scatter(
        delta.astype(jnp.float32).astype(jnp.bfloat16), "rep", scatter_dimension=0, tiled=True
    ).astype(jnp.float32)
    summed = lax.all_to_all(
        summed.astype(jnp.bfloat16), TP, split_axis=0, concat_axis=1, tiled=True
    ).astype(summed.dtype)
    average = summed / replicas
    new_momentum = nesterov * momentum + average
    new_outer = outer_weights - outer_rate * (average + nesterov * new_momentum)
    rounded = new_outer.astype(jnp.bfloat16)
    part = lax.all_to_all(rounded, TP, split_axis=1, concat_axis=0, tiled=True)
    weights = lax.all_gather(part, "rep", axis=0, tiled=True)
    return (weights, new_outer, new_momentum)


def solution(mesh):
    split = Mesh(mesh.devices.reshape(mesh.shape["rep"], 4, 4), ("rep", "tp_0", "tp_1"))
    in_specs = (
        P("rep", TP, None),
        P("rep", None, TP),
        P("rep", None, TP),
        P(REP_TP, None),
        P(REP_TP, None),
    )
    out_specs = (P(None, TP), P(REP_TP, None), P(REP_TP, None))
    return jax.shard_map(
        on_device, mesh=split, in_specs=in_specs, out_specs=out_specs, check_vma=False
    )
```

profile of v0, /device:TPU:1, one launch (start us, length us, event | category | flops | bytes accessed | tf_op | source)
XLA Modules:
  0.0 488.0 jit_solution(10202288569812770123)
XLA Ops:
  7.2 0.0 copy-start
  7.2 0.0 all-gather.4.cloned.1.call-start
  7.2 0.7 all-gather.4.cloned.1.call-update
  7.9 0.0 all-gather.6.cloned.1.call-start
  8.0 89.4 %all-gather.4.cloned.1.call-done = bf16[1,512,4096]{2,1,0:T(8,128)(2,1)} async-done(((bf16[1,128,4096]{2,1,0:T(8,128)(2,1)}), bf16[1,512,4096]{2,1,0:T(8,128)(2,1)}) %all-gather.4.cloned.1.call-update) | async-done | bytes 4194320 | tf_op jit(solution)/shard_map/all_gather | solution.py:16
  97.4 0.0 all-gather.6.cloned.1.call-update
  97.4 0.0 reduce-scatter.2.cloned.1.call-start
  97.4 158.5 %all-gather.6.cloned.1.call-done = bf16[1,2048,4096]{2,1,0:T(8,128)(2,1)} async-done(((bf16[1,512,4096]{2,1,0:T(8,128)(2,1)}), bf16[1,2048,4096]{2,1,0:T(8,128)(2,1)}) %all-gather.6.cloned.1.call-update) | async-done | bytes 16777232 | tf_op jit(solution)/shard_map/all_gather | solution.py:16
  255.9 0.0 copy-done
  255.9 14.4 %fusion.2 = bf16[4096,512]{1,0:T(8,128)(2,1)} fusion(bf16[1,2048,4096]{2,1,0:T(8,128)(2,1)} %all-gather.6.cloned.1.call-done, bf16[1,4096,512]{2,1,0:T(8,128)(2,1)} %param.7, bf16[1,2048,512]{2,1,0:T(8,128)(2,1)S(1)} %copy-done), kind=kOutput, calls=%fused_computation.3 | convolution fusion | flops 8596226048 | bytes 27262976 | tf_op jit(solution)/shard_map/td,tf->df/dot_general | solution.py:23
  270.4 0.0 copy-start.1
  270.4 0.0 copy-start.2
  270.4 0.0 reduce-scatter.2.cloned.1.call-update
  270.4 0.0 all-gather.8.cloned.1.call-start
  270.4 103.5 %reduce-scatter.2.cloned.1.call-done = bf16[256,512]{1,0:T(8,128)(2,1)} async-done(((bf16[4096,512]{1,0:T(8,128)(2,1)}), bf16[256,512]{1,0:T(8,128)(2,1)}) %reduce-scatter.2.cloned.1.call-update) | async-done | bytes 262160 | tf_op jit(solution)/shard_map/reduce_scatter | solution.py:30
  374.0 12.9 %all_to_all.32 = bf16[16,16,512]{2,1,0:T(8,128)(2,1)S(1)} all-to-all(bf16[16,16,512]{2,1,0:T(8,128)(2,1)} %bitcast.27), channel_id=1, replica_groups=mesh['rep'=16,'tp_0'=4,'tp_1'=4] {'tp_0','tp_1'}, dimensions={0} | all-to-all | bytes 524288 | tf_op jit(solution)/shard_map/all_to_all | solution.py:33
  386.9 0.1 multiply_bitcast_fusion
  387.0 0.0 copy-done.1
  387.0 0.0 copy-done.2
  387.0 1.1 fusion.6
  388.1 11.3 %all_to_all.33 = bf16[16,16,512]{2,0,1:T(8,128)(2,1)} all-to-all(bf16[16,16,512]{2,0,1:T(8,128)(2,1)S(1)} %bitcast.25), channel_id=1, replica_groups=mesh['rep'=16,'tp_0'=4,'tp_1'=4] {'tp_0','tp_1'}, dimensions={1} | all-to-all | bytes 524288 | tf_op jit(solution)/shard_map/all_to_all | solution.py:40
  399.4 0.0 all-gather.8.cloned.1.call-update
  399.5 77.6 %all-gather.8.cloned.1.call-done = bf16[4096,512]{1,0:T(8,128)(2,1)} async-done(((bf16[256,512]{1,0:T(8,128)(2,1)}), bf16[4096,512]{1,0:T(8,128)(2,1)}) %all-gather.8.cloned.1.call-update) | async-done | bytes 4194320 | tf_op jit(solution)/shard_map/all_gather | solution.py:41
  477.0 4.5 copy.18
  (2 shorter events, 0.1 us)
Async XLA Ops:
  7.2 248.8 %copy-start = (bf16[1,2048,512]{2,1,0:T(8,128)(2,1)S(1)}, bf16[1,2048,512]{2,1,0:T(8,128)(2,1)}, u32[]{:S(2)}) copy-start(bf16[1,2048,512]{2,1,0:T(8,128)(2,1)} %param.6) | copy-start | bytes 6291460
  7.2 90.2 %all-gather.4.cloned.1.call-start = ((), (), s32[]{:S(2)}) async-start(), calls=%async_computation.3 | async-start | bytes 5242880 | tf_op jit(solution)/shard_map/all_gather | solution.py:16
  7.9 248.0 %all-gather.6.cloned.1.call-start = ((), (), s32[]{:S(2)}) async-start(), calls=%async_computation.4 | async-start | bytes 20971520 | tf_op jit(solution)/shard_map/all_gather | solution.py:16
  97.4 276.6 %reduce-scatter.2.cloned.1.call-start = ((), (), s32[]{:S(2)}) async-start(), calls=%async_computation.5 | async-start | bytes 4456448 | tf_op jit(solution)/shard_map/reduce_scatter | solution.py:30
  270.4 116.6 %copy-start.1 = (f32[16,8192]{1,0:T(8,128)S(1)}, f32[16,8192]{1,0:T(8,128)}, u32[]{:S(2)}) copy-start(f32[16,8192]{1,0:T(8,128)} %param.8) | copy-start | bytes 1572868
  270.4 116.6 %copy-start.2 = (f32[16,8192]{1,0:T(8,128)S(1)}, f32[16,8192]{1,0:T(8,128)}, u32[]{:S(2)}) copy-start(f32[16,8192]{1,0:T(8,128)} %param.9) | copy-start | bytes 1572868
  270.4 206.6 %all-gather.8.cloned.1.call-start = ((), (), s32[]{:S(2)}) async-start(), calls=%async_computation.6 | async-start | bytes 4456448 | tf_op jit(solution)/shard_map/all_gather | solution.py:41
Sparse Core Ops, SparseCore 0:
  9.8 87.5 all-gather.3
  99.2 156.7 all-gather.5
  270.5 103.4 reduce-scatter.1
  399.6 77.4 all-gather.7
where the time goes:
time: 488 us
  waiting for transfers between devices  430 us (88%)
  blocking collectives  24.2 us (5%)
  matrix products  14.4 us (3%)
  between operations  13.8 us (3%)
    all_gather x2, waiting for transfers between devices, gathered_by_axis(): nearer = lax.all_gather(shard, axes[-1], axis=dim, tiled=True)  248 us
    reduce_scatter x1, waiting for transfers between devices, on_device(): lax.psum_scatter(delta.astype(jnp.float32).astype(jnp.bfloat16), 'rep', s...  104 us
    all_gather x1, waiting for transfers between devices, on_device(): weights = lax.all_gather(part, 'rep', axis=0, tiled=True)  77.6 us
    dot_general x1, matrix products, on_device(): jnp.einsum('td,tf->df', gathered_by_axis(activations, TP, 1)[0], cot_rows...  14.4 us
    all_to_all x1, blocking collectives, on_device(): lax.all_to_all(summed.astype(jnp.bfloat16), TP, split_axis=0, concat_axis...  12.9 us
    all_to_all x1, blocking collectives, on_device(): part = lax.all_to_all(rounded, TP, split_axis=1, concat_axis=0, tiled=True)  11.3 us
  transfers between devices with their start and end apart: 4, of which 4 were waited for; matrix products, arithmetic and copies ran while one was open for 0% of the time, Pallas kernels for 0%

commit v1 on v0

--- a/solution.py
+++ b/solution.py
@@ -38,7 +38,9 @@
     new_outer = outer_weights - outer_rate * (average + nesterov * new_momentum)
     rounded = new_outer.astype(jnp.bfloat16)
     part = lax.all_to_all(rounded, TP, split_axis=1, concat_axis=0, tiled=True)
-    weights = lax.all_gather(part, "rep", axis=0, tiled=True)
+    weights = jnp.concatenate(
+        lax.all_to_all(jnp.stack([part] * lax.axis_size("rep")), "rep", 0, 0), axis=0
+    )
     return (weights, new_outer, new_momentum)
 
 

time: 488 us -> 516 us (1.057)
  blocking collectives: 24.2 us -> 128 us
  waiting for transfers between devices: 430 us -> 352 us
    all_to_all x0 -> x1, blocking collectives: none -> 104 us  [on_device(): lax.all_to_all(jnp.stack([part] * lax.axis_size('rep')), 'rep', 0, 0)]
    all_gather x1 -> x0, waiting for transfers between devices: 77.6 us -> none  [on_device(): weights = lax.all_gather(part, 'rep', axis=0, tiled=True)]
  transfers between devices with their start and end apart: 4 -> 3, of which waited for: 4 -> 3; matrix products, arithmetic and copies ran while one was open for 0% -> 0% of each run, Pallas kernels for 0% -> 0%
where the time goes in v1:
time: 516 us; the launch traced here: 513 us
  waiting for transfers between devices  352 us (68%)
  blocking collectives  128 us (25%)
  matrix products  14.4 us (3%)
  between operations  13.8 us (3%)
    all_gather x2, waiting for transfers between devices, gathered_by_axis(): nearer = lax.all_gather(shard, axes[-1], axis=dim, tiled=True)  248 us
    all_to_all x1, blocking collectives, on_device(): lax.all_to_all(jnp.stack([part] * lax.axis_size('rep')), 'rep', 0, 0)  104 us
    reduce_scatter x1, waiting for transfers between devices, on_device(): lax.psum_scatter(delta.astype(jnp.float32).astype(jnp.bfloat16), 'rep', s...  104 us
    dot_general x1, matrix products, on_device(): jnp.einsum('td,tf->df', gathered_by_axis(activations, TP, 1)[0], cot_rows...  14.4 us
    all_to_all x1, blocking collectives, on_device(): lax.all_to_all(summed.astype(jnp.bfloat16), TP, split_axis=0, concat_axis...  12.9 us
    all_to_all x1, blocking collectives, on_device(): part = lax.all_to_all(rounded, TP, split_axis=1, concat_axis=0, tiled=True)  11.3 us
  transfers between devices with their start and end apart: 3, of which 3 were waited for; matrix products, arithmetic and copies ran while one was open for 0% of the time, Pallas kernels for 0%

profile of v1, /device:TPU:1, one launch (start us, length us, event | category | flops | bytes accessed | tf_op | source)
XLA Modules:
  0.0 512.7 jit_solution(13424773250323593053)
XLA Ops:
  7.2 0.0 copy-start
  7.2 0.0 all-gather.3.cloned.1.call-start
  7.2 0.7 all-gather.3.cloned.1.call-update
  7.9 0.0 all-gather.5.cloned.1.call-start
  8.0 89.4 %all-gather.3.cloned.1.call-done = bf16[1,512,4096]{2,1,0:T(8,128)(2,1)} async-done(((bf16[1,128,4096]{2,1,0:T(8,128)(2,1)}), bf16[1,512,4096]{2,1,0:T(8,128)(2,1)}) %all-gather.3.cloned.1.call-update) | async-done | bytes 4194320 | tf_op jit(solution)/shard_map/all_gather | solution.py:16
  97.4 0.0 all-gather.5.cloned.1.call-update
  97.4 0.0 reduce-scatter.2.cloned.1.call-start
  97.4 158.5 %all-gather.5.cloned.1.call-done = bf16[1,2048,4096]{2,1,0:T(8,128)(2,1)} async-done(((bf16[1,512,4096]{2,1,0:T(8,128)(2,1)}), bf16[1,2048,4096]{2,1,0:T(8,128)(2,1)}) %all-gather.5.cloned.1.call-update) | async-done | bytes 16777232 | tf_op jit(solution)/shard_map/all_gather | solution.py:16
  255.9 0.0 copy-done
  255.9 14.4 %fusion.2 = bf16[4096,512]{1,0:T(8,128)(2,1)} fusion(bf16[1,2048,4096]{2,1,0:T(8,128)(2,1)} %all-gather.5.cloned.1.call-done, bf16[1,4096,512]{2,1,0:T(8,128)(2,1)} %param.7, bf16[1,2048,512]{2,1,0:T(8,128)(2,1)S(1)} %copy-done), kind=kOutput, calls=%fused_computation.3 | convolution fusion | flops 8596226048 | bytes 27262976 | tf_op jit(solution)/shard_map/td,tf->df/dot_general | solution.py:23
  270.4 0.0 copy-start.1
  270.4 0.0 copy-start.2
  270.4 0.0 reduce-scatter.2.cloned.1.call-update
  270.4 103.6 %reduce-scatter.2.cloned.1.call-done = bf16[256,512]{1,0:T(8,128)(2,1)} async-done(((bf16[4096,512]{1,0:T(8,128)(2,1)}), bf16[256,512]{1,0:T(8,128)(2,1)}) %reduce-scatter.2.cloned.1.call-update) | async-done | bytes 262160 | tf_op jit(solution)/shard_map/reduce_scatter | solution.py:30
  374.0 12.9 %all_to_all.34 = bf16[16,16,512]{2,1,0:T(8,128)(2,1)S(1)} all-to-all(bf16[16,16,512]{2,1,0:T(8,128)(2,1)} %bitcast.29), channel_id=1, replica_groups=mesh['rep'=16,'tp_0'=4,'tp_1'=4] {'tp_0','tp_1'}, dimensions={0} | all-to-all | bytes 524288 | tf_op jit(solution)/shard_map/all_to_all | solution.py:33
  386.9 0.1 multiply_bitcast_fusion
  387.0 0.0 copy-done.1
  387.0 0.0 copy-done.2
  387.0 1.1 fusion.6
  388.1 11.3 %all_to_all.35 = bf16[16,16,512]{2,0,1:T(8,128)(2,1)S(1)} all-to-all(bf16[16,16,512]{2,0,1:T(8,128)(2,1)S(1)} %bitcast.27), channel_id=1, replica_groups=mesh['rep'=16,'tp_0'=4,'tp_1'=4] {'tp_0','tp_1'}, dimensions={1} | all-to-all | bytes 524288 | tf_op jit(solution)/shard_map/all_to_all | solution.py:40
  399.4 0.4 stack.5
  399.8 104.3 %all_to_all.36 = bf16[16,256,512]{2,1,0:T(8,128)(2,1)S(1)} all-to-all(bf16[16,256,512]{2,1,0:T(8,128)(2,1)S(1)} %stack.5), channel_id=1, replica_groups=mesh['rep'=16,'tp_0'=4,'tp_1'=4] {'rep'}, dimensions={0} | all-to-all | bytes 8388608 | tf_op jit(solution)/shard_map/all_to_all | solution.py:42
  504.1 2.0 copy.19
  (2 shorter events, 0.1 us)
Async XLA Ops:
  7.2 248.8 %copy-start = (bf16[1,2048,512]{2,1,0:T(8,128)(2,1)S(1)}, bf16[1,2048,512]{2,1,0:T(8,128)(2,1)}, u32[]{:S(2)}) copy-start(bf16[1,2048,512]{2,1,0:T(8,128)(2,1)} %param.6) | copy-start | bytes 6291460
  7.2 90.2 %all-gather.3.cloned.1.call-start = ((), (), s32[]{:S(2)}) async-start(), calls=%async_computation.4 | async-start | bytes 5242880 | tf_op jit(solution)/shard_map/all_gather | solution.py:16
  7.9 248.0 %all-gather.5.cloned.1.call-start = ((), (), s32[]{:S(2)}) async-start(), calls=%async_computation.5 | async-start | bytes 20971520 | tf_op jit(solution)/shard_map/all_gather | solution.py:16
  97.4 276.6 %reduce-scatter.2.cloned.1.call-start = ((), (), s32[]{:S(2)}) async-start(), calls=%async_computation.6 | async-start | bytes 4456448 | tf_op jit(solution)/shard_map/reduce_scatter | solution.py:30
  270.4 116.6 %copy-start.1 = (f32[16,8192]{1,0:T(8,128)S(1)}, f32[16,8192]{1,0:T(8,128)}, u32[]{:S(2)}) copy-start(f32[16,8192]{1,0:T(8,128)} %param.8) | copy-start | bytes 1572868
  270.4 116.6 %copy-start.2 = (f32[16,8192]{1,0:T(8,128)S(1)}, f32[16,8192]{1,0:T(8,128)}, u32[]{:S(2)}) copy-start(f32[16,8192]{1,0:T(8,128)} %param.9) | copy-start | bytes 1572868
Sparse Core Ops, SparseCore 0:
  9.8 87.5 all-gather.2
  99.2 156.7 all-gather.4
  270.5 103.4 reduce-scatter.1
